TPU v7x, 32 devices: a whole 2x2x4 slice. The times are simulated.
32 devices in a mesh: dp: 8 (over z, x), mp: 4 (over y, core).
Axes of the slice: x: 2, y: 2, z: 4, core: 2. Of those that a mesh axis runs over, the one named last changes fastest.
Arguments:
- gating_logits: bfloat16 [8, 3, 64, 7168], P('dp', None, None, 'mp'), may hold values from -6 to 6
- lifted_hidden_values: bfloat16 [8, 3, 64, 7168], P('dp', None, None, 'mp'), may hold values from -6 to 6
- loss_output_grad: bfloat16 [8, 3, 64, 2048], P('dp', None, None, 'mp'), may hold values from -160 to 160
- arrival_flags: int32 [8], P('dp'), may hold values from 0 to 1, as said below
- block_owner_map: int32 [8, 3], P('dp'), may hold values from 0 to 7, as said below
- decoder_multipliers: int32 [8, 3], P('dp'), may hold values from 1 to 4
- block_piece_number: int32 [8], replicated, may hold values from 1 to 2, as said below
Outputs:
- down_grad: float32 [2048, 7168], P('dp', 'mp')
Inputs may be any that keep to these rules, and one draw needn't show every extreme that they name: `arrival_flags`: at least one replica survives. `block_owner_map`: row i lists the partitions (i + r + k) mod 8 for k < 3, with one r for all rows. `block_piece_number`: some partition has exactly 2 live tiles.
All inputs are finite; a program needn't handle non-finite values.
Results may differ from a plain program's by a relative error of at most 0.0042.
Values may be sent and summed in bfloat16 or wider, within the bound.
No kernel may reach another device: no remote copies, remote signals or barrier semaphores. Data moves between devices by JAX's collectives and lax.ppermute only.
A program may use at most 128 MiB of HBM per device.

v0:
```python
import jax
import jax.numpy as jnp
from jax import lax
from jax.sharding import PartitionSpec as P

TILE = 32
CHUNKS = 2


def project(cots, hs):
    return lax.dot_general(cots, hs, (((0,), (0,)), ((), ())), preferred_element_type=jnp.float32)


def on_device(gate, up, cot, flags, owner, mult, pieces):
    _, slots, tok, cols = gate.shape
    feats = cot.shape[3]
    dp = lax.axis_size("dp")
    mp = lax.axis_size("mp")
    outer, inner = (mp, dp // mp)
    i = lax.axis_index("dp")
    z = i // inner
    x = i % inner
    ids = jnp.arange(pieces.shape[0], dtype=jnp.int32)
    tiles = jnp.sum(jnp.where(owner[0][:, None] == ids[None, :], pieces[None, :], 0), axis=1)
    live = tiles * TILE
    weight = flags[0].astype(jnp.float32) * mult[0].astype(jnp.float32)
    tokens = jnp.sum(weight * live.astype(jnp.float32))
    rows = slots * tok
    block = feats // inner
    scaled = (
        (cot[0].astype(jnp.float32) * weight[:, None, None])
        .astype(jnp.bfloat16)
        .reshape(rows, feats)
    )
    if inner == 2:
        swapped = jnp.concatenate([scaled[:, block:], scaled[:, :block]], axis=1)
        scaled = jnp.where(x == 0, scaled, swapped)
    both = ("dp", "mp")
    perm = []
    for a in range(outer):
        for b in range(inner):
            for m in range(mp):
                perm.append(((a * inner + b) * mp + m, (m * inner + b) * mp + (a ^ m)))
    moved = lax.ppermute(scaled, both, perm)
    cots = lax.all_gather(moved, "mp", axis=0, tiled=True)
    total = lax.psum(tokens, "dp")

    def perm_z(pairs):
        return [(a * inner + b, c * inner + b) for a, c in pairs for b in range(inner)]

    sizes = [cols // CHUNKS] * CHUNKS
    lo = 0
    mask = jnp.arange(tok, dtype=jnp.int32)[None, :] < live[:, None]
    outs = []
    for c, w in enumerate(sizes):
        g = gate[0, :, :, lo : lo + w].astype(jnp.float32)
        u = up[0, :, :, lo : lo + w].astype(jnp.float32)
        lo += w
        h = (
            (jax.nn.silu(g) * u * mask[:, :, None].astype(jnp.float32))
            .astype(jnp.bfloat16)
            .reshape(rows, w)
        )
        ha = lax.ppermute(h, "dp", perm_z([(0, 1), (1, 0), (2, 3), (3, 2)]))
        hq = lax.ppermute(h, "dp", perm_z([(0, 2), (2, 0), (1, 3), (3, 1)]))
        hf1 = lax.ppermute(h, "dp", perm_z([(1, 2), (2, 1)]))
        hf2 = lax.ppermute(hq, "dp", perm_z([(1, 0), (2, 3)]))
        hf = jnp.where((z == 1) | (z == 2), hf1, hf2)
        hs = jnp.concatenate([h, ha, hq, hf], axis=0)
        if inner == 2:
            send = project(cots[:, block:], hs).astype(jnp.bfloat16)
            got = lax.ppermute(send, "dp", [(d, d ^ 1) for d in range(dp)])
            outs.append((project(cots[:, :block], hs) + got.astype(jnp.float32)) / total)
        else:
            partial = project(cots, hs).astype(jnp.bfloat16).reshape(inner, block, w)
            groups = [[a * inner + b for b in range(inner)] for a in range(outer)]
            got = lax.all_to_all(partial, "dp", 0, 0, axis_index_groups=groups, tiled=True)
            outs.append(jnp.sum(got.astype(jnp.float32), axis=0) / total)
    return jnp.concatenate(outs, axis=1)


def solution(mesh):
    return jax.shard_map(
        on_device,
        mesh=mesh,
        in_specs=(
            P("dp", None, None, "mp"),
            P("dp", None, None, "mp"),
            P("dp", None, None, "mp"),
            P("dp"),
            P("dp", None),
            P("dp", None),
            P(),
        ),
        out_specs=P("dp", "mp"),
        check_vma=False,
    )
```

profile of v0, /device:TPU:4, one launch (start us, length us, event | category | flops | bytes accessed | tf_op | source)
XLA Modules:
  0.0 109.4 jit_solution(2149252115974620749)
XLA Ops:
  0.0 0.9 select_reduce_fusion
  0.9 0.1 fusion.19
  0.9 0.1 reshape.63
  1.0 1.4 %fusion.24 = (bf16[1,3,64,896]{3,2,1,0:T(8,128)(2,1)S(1)}, bf16[1,3,64,896]{3,2,1,0:T(8,128)(2,1)S(1)}, bf16[1,3,64,896]{3,2,1,0:T(8,128)(2,1)S(1)}, bf16[1,3,64,896]{3,2,1,0:T(8,128)(2,1)S(1)}) fusion(bf16[1,3,64,1792]{3,2,1,0:T(8,128)(2,1)} %param.7, bf16[1,3,64,1792]{3,2,1,0:T(8,128)(2,1)} %param.8), kind=kLoop, calls=%fused_computation.45 | loop fusion | bytes 2752512 | tf_op jit(solution)/shard_map/slice | solution.py:56
  2.5 0.6 fusion.13
  3.1 2.7 %collective-permute-start.2 = (bf16[192,896]{1,0:T(8,128)(2,1)S(1)}, bf16[192,896]{1,0:T(8,128)(2,1)S(1)}, u32[]{:S(2)}, u32[]{:S(2)}) collective-permute-start(bf16[192,896]{1,0:T(8,128)(2,1)S(1)} %get-tuple-element.13), channel_id=1, source_target_pairs={{0,16},{4,20},{16,0},{20,4},{8,24},{12,28},{24,8},{28,12},{1,17},{... | collective-permute-start | bytes 1032200 | tf_op jit(solution)/shard_map/ppermute | solution.py:65
  6.4 0.6 multiply_reduce_fusion
  7.0 0.1 mul.72
  7.0 0.1 mul.73
  7.1 0.1 fusion.14
  7.2 0.1 maximum_select_fusion
  7.4 2.2 %collective-permute-start = (bf16[192,512]{1,0:T(8,128)(2,1)S(1)}, bf16[192,512]{1,0:T(8,128)(2,1)S(1)}, u32[]{:S(2)}, u32[]{:S(2)}) collective-permute-start(bf16[192,512]{1,0:T(8,128)(2,1)S(1)} %maximum_select_fusion), channel_id=1, source_target_pairs={{0,0},{1,9},{2,18},{3,27},{4,4},{5,13},{6,22},{7,31},{8,1},{9,8},{... | collective-permute-start | bytes 589832 | tf_op jit(solution)/shard_map/ppermute | solution.py:44
  9.6 0.7 collective-permute-start.3
  10.3 4.0 %collective-permute-start.7 = (bf16[192,896]{1,0:T(8,128)(2,1)S(1)}, bf16[192,896]{1,0:T(8,128)(2,1)}, u32[]{:S(2)}, u32[]{:S(2)}) collective-permute-start(bf16[192,896]{1,0:T(8,128)(2,1)S(1)} %get-tuple-element.14), channel_id=1, source_target_pairs={{0,16},{4,20},{16,0},{20,4},{8,24},{12,28},{24,8},{28,12},{1,17},{... | collective-permute-start | bytes 1032200 | tf_op jit(solution)/shard_map/ppermute | solution.py:65
  14.3 15.4 %collective-permute-done.2 = bf16[192,896]{1,0:T(8,128)(2,1)S(1)} collective-permute-done((bf16[192,896]{1,0:T(8,128)(2,1)S(1)}, bf16[192,896]{1,0:T(8,128)(2,1)S(1)}, u32[]{:S(2)}, u32[]{:S(2)}) %collective-permute-start.2) | collective-permute-done | bytes 344096 | tf_op jit(solution)/shard_map/ppermute | solution.py:65
  29.7 1.3 %collective-permute-start.4 = (bf16[192,896]{1,0:T(8,128)(2,1)S(1)}, bf16[192,896]{1,0:T(8,128)(2,1)S(1)}, u32[]{:S(2)}, u32[]{:S(2)}) collective-permute-start(bf16[192,896]{1,0:T(8,128)(2,1)S(1)} %collective-permute-done.2), channel_id=1, source_target_pairs={{8,0},{12,4},{16,24},{20,28},{9,1},{13,5},{17,25},{21,29},{10,2},{... | collective-permute-start | bytes 1032200 | tf_op jit(solution)/shard_map/ppermute | solution.py:67
  31.0 4.0 %collective-permute-start.1 = (bf16[192,896]{1,0:T(8,128)(2,1)S(1)}, bf16[192,896]{1,0:T(8,128)(2,1)}, u32[]{:S(2)}, u32[]{:S(2)}) collective-permute-start(bf16[192,896]{1,0:T(8,128)(2,1)S(1)} %get-tuple-element.13), channel_id=1, source_target_pairs={{0,8},{4,12},{8,0},{12,4},{16,24},{20,28},{24,16},{28,20},{1,9},{5... | collective-permute-start | bytes 1032200 | tf_op jit(solution)/shard_map/ppermute | solution.py:64
  34.9 2.8 %collective-permute-done = bf16[192,512]{1,0:T(8,128)(2,1)S(1)} collective-permute-done((bf16[192,512]{1,0:T(8,128)(2,1)S(1)}, bf16[192,512]{1,0:T(8,128)(2,1)S(1)}, u32[]{:S(2)}, u32[]{:S(2)}) %collective-permute-start) | collective-permute-done | bytes 196640 | tf_op jit(solution)/shard_map/ppermute | solution.py:44
  37.8 0.7 collective-permute-start.8
  38.4 7.5 %all_gather.3 = bf16[768,512]{1,0:T(8,128)(2,1)S(1)} all-gather(bf16[192,512]{1,0:T(8,128)(2,1)S(1)} %collective-permute-done), channel_id=1, replica_groups=mesh['dp'=8,'mp'=4] {'mp'}, dimensions={0}, use_global_device_ids=true | all-gather | bytes 983040 | tf_op jit(solution)/shard_map/all_gather | solution.py:45
  45.9 4.2 %collective-permute-start.6 = (bf16[192,896]{1,0:T(8,128)(2,1)S(1)}, bf16[192,896]{1,0:T(8,128)(2,1)S(1)}, u32[]{:S(2)}, u32[]{:S(2)}) collective-permute-start(bf16[192,896]{1,0:T(8,128)(2,1)S(1)} %get-tuple-element.14), channel_id=1, source_target_pairs={{0,8},{4,12},{8,0},{12,4},{16,24},{20,28},{24,16},{28,20},{1,9},{5... | collective-permute-start | bytes 1032200 | tf_op jit(solution)/shard_map/ppermute | solution.py:64
  50.1 1.3 %collective-permute-start.9 = (bf16[192,896]{1,0:T(8,128)(2,1)}, bf16[192,896]{1,0:T(8,128)(2,1)S(1)}, u32[]{:S(2)}, u32[]{:S(2)}) collective-permute-start(bf16[192,896]{1,0:T(8,128)(2,1)} %collective-permute-done.7), channel_id=1, source_target_pairs={{8,0},{12,4},{16,24},{20,28},{9,1},{13,5},{17,25},{21,29},{10,2},{... | collective-permute-start | bytes 1032200 | tf_op jit(solution)/shard_map/ppermute | solution.py:67
  51.4 6.4 %collective-permute-done.1 = bf16[192,896]{1,0:T(8,128)(2,1)} collective-permute-done((bf16[192,896]{1,0:T(8,128)(2,1)S(1)}, bf16[192,896]{1,0:T(8,128)(2,1)}, u32[]{:S(2)}, u32[]{:S(2)}) %collective-permute-start.1) | collective-permute-done | bytes 344096 | tf_op jit(solution)/shard_map/ppermute | solution.py:64
  57.8 1.6 %convolution_convert_fusion.1 = bf16[256,896]{1,0:T(8,128)(2,1)S(1)} fusion(bf16[768,512]{1,0:T(8,128)(2,1)S(1)} %all_gather.3, bf16[192,896]{1,0:T(8,128)(2,1)S(1)} %broadcast_select_fusion.1, bf16[192,896]{1,0:T(8,128)(2,1)S(1)} %collective-permute-done.2, bf16[192,896]{1,0:T(8,128)(2,1)} %collective-permute-done.1, bf16[192,896]{1,0:T(8,128)(2,1)S(1)} %get-tuple-element.13), kind=kOutput, calls=%fused_computation.8 | convolution fusion | flops 358055936 | bytes 2228224 | tf_op jit(solution)/shard_map/dot_general | solution.py:11
  59.4 1.6 %collective-permute-start.5 = (bf16[256,896]{1,0:T(8,128)(2,1)S(1)}, bf16[256,896]{1,0:T(8,128)(2,1)S(1)}, u32[]{:S(2)}, u32[]{:S(2)}) collective-permute-start(bf16[256,896]{1,0:T(8,128)(2,1)S(1)} %convolution_convert_fusion.1), channel_id=1, source_target_pairs={{0,4},{4,0},{8,12},{12,8},{16,20},{20,16},{24,28},{28,24},{1,5},{5... | collective-permute-start | bytes 1376264 | tf_op jit(solution)/shard_map/ppermute | solution.py:72
  61.0 11.1 %collective-permute-done.9 = bf16[192,896]{1,0:T(8,128)(2,1)S(1)} collective-permute-done((bf16[192,896]{1,0:T(8,128)(2,1)}, bf16[192,896]{1,0:T(8,128)(2,1)S(1)}, u32[]{:S(2)}, u32[]{:S(2)}) %collective-permute-start.9) | collective-permute-done | bytes 344096 | tf_op jit(solution)/shard_map/ppermute | solution.py:67
  72.2 2.5 %convolution_convert_fusion = bf16[256,896]{1,0:T(8,128)(2,1)} fusion(bf16[768,512]{1,0:T(8,128)(2,1)S(1)} %all_gather.3, bf16[192,896]{1,0:T(8,128)(2,1)S(1)} %broadcast_select_fusion, bf16[192,896]{1,0:T(8,128)(2,1)} %collective-permute-done.7, bf16[192,896]{1,0:T(8,128)(2,1)S(1)} %collective-permute-done.6, bf16[192,896]{1,0:T(8,128)(2,1)S(1)} %get-tuple-element.14), kind=kOutput, calls=%fused_computation.7 | convolution fusion | flops 358055936 | bytes 2228224 | tf_op jit(solution)/shard_map/dot_general | solution.py:11
  74.7 1.5 %collective-permute-start.10 = (bf16[256,896]{1,0:T(8,128)(2,1)}, bf16[256,896]{1,0:T(8,128)(2,1)}, u32[]{:S(2)}, u32[]{:S(2)}) collective-permute-start(bf16[256,896]{1,0:T(8,128)(2,1)} %convolution_convert_fusion), channel_id=1, source_target_pairs={{0,4},{4,0},{8,12},{12,8},{16,20},{20,16},{24,28},{28,24},{1,5},{5... | collective-permute-start | bytes 1376264 | tf_op jit(solution)/shard_map/ppermute | solution.py:72
  76.2 27.1 %psum.7 = f32[]{:T(128)} all-reduce(f32[]{:T(128)} %get-tuple-element.5), channel_id=1, replica_groups=mesh['dp'=8,'mp'=4] {'dp'}, use_global_device_ids=true, to_apply=%region_2.3 | all-reduce | flops 1 | bytes 8 | tf_op jit(solution)/shard_map/psum | solution.py:46
  103.3 2.3 %fusion.1 = f32[256,896]{1,0:T(8,128)S(1)} fusion(bf16[256,896]{1,0:T(8,128)(2,1)S(1)} %collective-permute-done.5, f32[]{:T(128)} %psum.7, bf16[768,512]{1,0:T(8,128)(2,1)S(1)} %all_gather.3, bf16[192,896]{1,0:T(8,128)(2,1)S(1)} %broadcast_select_fusion.1, bf16[192,896]{1,0:T(8,128)(2,1)S(1)} %copy-done.3, bf16[192,896]{1,0:T(8,128)(2,1)} %collective-permute-done.1, ...), kind=kOutput, calls=%fused_computation.6 | convolution fusion | flops 358514688 | bytes 3145732 | tf_op jit(solution)/shard_map/dot_general | solution.py:11
  105.6 2.4 %fusion = f32[256,896]{1,0:T(8,128)S(1)} fusion(bf16[256,896]{1,0:T(8,128)(2,1)} %collective-permute-done.10, f32[]{:T(128)} %psum.7, bf16[768,512]{1,0:T(8,128)(2,1)S(1)} %all_gather.3, bf16[192,896]{1,0:T(8,128)(2,1)S(1)} %broadcast_select_fusion, bf16[192,896]{1,0:T(8,128)(2,1)} %collective-permute-done.7, bf16[192,896]{1,0:T(8,128)(2,1)S(1)} %copy-done.5, ...), kind=kOutput, calls=%fused_computation.4 | convolution fusion | flops 358514688 | bytes 3145732 | tf_op jit(solution)/shard_map/dot_general | solution.py:11
  108.0 1.4 %pad_maximum_fusion = f32[256,1792]{1,0:T(8,128)} fusion(f32[256,896]{1,0:T(8,128)S(1)} %fusion, f32[256,896]{1,0:T(8,128)S(1)} %fusion.1), kind=kLoop, calls=%fused_computation | loop fusion | flops 458752 | bytes 3670016 | tf_op jit(solution)/shard_map/concatenate | solution.py:79
  (23 shorter events, 0.1 us)
Async XLA Ops:
  1.0 5.4 %copy-start.1 = (s32[1,3]{1,0:T(1,128)S(1)}, s32[1,3]{1,0:T(1,128)}, u32[]{:S(2)}) copy-start(s32[1,3]{1,0:T(1,128)} %param.12) | copy-start | bytes 40
  1.0 6.1 %copy-start = (bf16[1,3,64,512]{3,2,1,0:T(8,128)(2,1)S(1)}, bf16[1,3,64,512]{3,2,1,0:T(8,128)(2,1)}, u32[]{:S(2)}) copy-start(bf16[1,3,64,512]{3,2,1,0:T(8,128)(2,1)} %param.9) | copy-start | bytes 589828
  3.1 26.6 %collective-permute-start.2 = (bf16[192,896]{1,0:T(8,128)(2,1)S(1)}, bf16[192,896]{1,0:T(8,128)(2,1)S(1)}, u32[]{:S(2)}, u32[]{:S(2)}) collective-permute-start(bf16[192,896]{1,0:T(8,128)(2,1)S(1)} %get-tuple-element.13), channel_id=1, source_target_pairs={{0,16},{4,20},{16,0},{20,4},{8,24},{12,28},{24,8},{28,12},{1,17},{... | collective-permute-start | bytes 1032200 | tf_op jit(solution)/shard_map/ppermute | solution.py:65
  7.4 30.4 %collective-permute-start = (bf16[192,512]{1,0:T(8,128)(2,1)S(1)}, bf16[192,512]{1,0:T(8,128)(2,1)S(1)}, u32[]{:S(2)}, u32[]{:S(2)}) collective-permute-start(bf16[192,512]{1,0:T(8,128)(2,1)S(1)} %maximum_select_fusion), channel_id=1, source_target_pairs={{0,0},{1,9},{2,18},{3,27},{4,4},{5,13},{6,22},{7,31},{8,1},{9,8},{... | collective-permute-start | bytes 589832 | tf_op jit(solution)/shard_map/ppermute | solution.py:44
  9.6 36.3 %collective-permute-start.3 = (bf16[192,896]{1,0:T(8,128)(2,1)S(1)}, bf16[192,896]{1,0:T(8,128)(2,1)S(1)}, u32[]{:S(2)}, u32[]{:S(2)}) collective-permute-start(bf16[192,896]{1,0:T(8,128)(2,1)S(1)} %get-tuple-element.13), channel_id=1, source_target_pairs={{8,16},{12,20},{16,8},{20,12},{9,17},{13,21},{17,9},{21,13},{10,18... | collective-permute-start | bytes 1032200 | tf_op jit(solution)/shard_map/ppermute | solution.py:66
  10.3 39.7 %collective-permute-start.7 = (bf16[192,896]{1,0:T(8,128)(2,1)S(1)}, bf16[192,896]{1,0:T(8,128)(2,1)}, u32[]{:S(2)}, u32[]{:S(2)}) collective-permute-start(bf16[192,896]{1,0:T(8,128)(2,1)S(1)} %get-tuple-element.14), channel_id=1, source_target_pairs={{0,16},{4,20},{16,0},{20,4},{8,24},{12,28},{24,8},{28,12},{1,17},{... | collective-permute-start | bytes 1032200 | tf_op jit(solution)/shard_map/ppermute | solution.py:65
  29.7 28.1 %copy-start.2 = (bf16[192,896]{1,0:T(8,128)(2,1)}, bf16[192,896]{1,0:T(8,128)(2,1)S(1)}, u32[]{:S(2)}) copy-start(bf16[192,896]{1,0:T(8,128)(2,1)S(1)} %collective-permute-done.2) | copy-start | bytes 1032196
  29.7 21.7 %collective-permute-start.4 = (bf16[192,896]{1,0:T(8,128)(2,1)S(1)}, bf16[192,896]{1,0:T(8,128)(2,1)S(1)}, u32[]{:S(2)}, u32[]{:S(2)}) collective-permute-start(bf16[192,896]{1,0:T(8,128)(2,1)S(1)} %collective-permute-done.2), channel_id=1, source_target_pairs={{8,0},{12,4},{16,24},{20,28},{9,1},{13,5},{17,25},{21,29},{10,2},{... | collective-permute-start | bytes 1032200 | tf_op jit(solution)/shard_map/ppermute | solution.py:67
  31.0 26.8 %collective-permute-start.1 = (bf16[192,896]{1,0:T(8,128)(2,1)S(1)}, bf16[192,896]{1,0:T(8,128)(2,1)}, u32[]{:S(2)}, u32[]{:S(2)}) collective-permute-start(bf16[192,896]{1,0:T(8,128)(2,1)S(1)} %get-tuple-element.13), channel_id=1, source_target_pairs={{0,8},{4,12},{8,0},{12,4},{16,24},{20,28},{24,16},{28,20},{1,9},{5... | collective-permute-start | bytes 1032200 | tf_op jit(solution)/shard_map/ppermute | solution.py:64
  37.8 23.2 %collective-permute-start.8 = (bf16[192,896]{1,0:T(8,128)(2,1)S(1)}, bf16[192,896]{1,0:T(8,128)(2,1)S(1)}, u32[]{:S(2)}, u32[]{:S(2)}) collective-permute-start(bf16[192,896]{1,0:T(8,128)(2,1)S(1)} %get-tuple-element.14), channel_id=1, source_target_pairs={{8,16},{12,20},{16,8},{20,12},{9,17},{13,21},{17,9},{21,13},{10,18... | collective-permute-start | bytes 1032200 | tf_op jit(solution)/shard_map/ppermute | solution.py:66
  45.9 26.2 %collective-permute-start.6 = (bf16[192,896]{1,0:T(8,128)(2,1)S(1)}, bf16[192,896]{1,0:T(8,128)(2,1)S(1)}, u32[]{:S(2)}, u32[]{:S(2)}) collective-permute-start(bf16[192,896]{1,0:T(8,128)(2,1)S(1)} %get-tuple-element.14), channel_id=1, source_target_pairs={{0,8},{4,12},{8,0},{12,4},{16,24},{20,28},{24,16},{28,20},{1,9},{5... | collective-permute-start | bytes 1032200 | tf_op jit(solution)/shard_map/ppermute | solution.py:64
  50.1 22.0 %collective-permute-start.9 = (bf16[192,896]{1,0:T(8,128)(2,1)}, bf16[192,896]{1,0:T(8,128)(2,1)S(1)}, u32[]{:S(2)}, u32[]{:S(2)}) collective-permute-start(bf16[192,896]{1,0:T(8,128)(2,1)} %collective-permute-done.7), channel_id=1, source_target_pairs={{8,0},{12,4},{16,24},{20,28},{9,1},{13,5},{17,25},{21,29},{10,2},{... | collective-permute-start | bytes 1032200 | tf_op jit(solution)/shard_map/ppermute | solution.py:67
  59.4 43.9 %collective-permute-start.5 = (bf16[256,896]{1,0:T(8,128)(2,1)S(1)}, bf16[256,896]{1,0:T(8,128)(2,1)S(1)}, u32[]{:S(2)}, u32[]{:S(2)}) collective-permute-start(bf16[256,896]{1,0:T(8,128)(2,1)S(1)} %convolution_convert_fusion.1), channel_id=1, source_target_pairs={{0,4},{4,0},{8,12},{12,8},{16,20},{20,16},{24,28},{28,24},{1,5},{5... | collective-permute-start | bytes 1376264 | tf_op jit(solution)/shard_map/ppermute | solution.py:72
  72.1 31.1 %copy-start.3 = (bf16[192,896]{1,0:T(8,128)(2,1)S(1)}, bf16[192,896]{1,0:T(8,128)(2,1)}, u32[]{:S(2)}) copy-start(bf16[192,896]{1,0:T(8,128)(2,1)} %copy-done.2) | copy-start | bytes 1032196
  72.2 2.5 %copy-start.4 = (bf16[192,896]{1,0:T(8,128)(2,1)}, bf16[192,896]{1,0:T(8,128)(2,1)S(1)}, u32[]{:S(2)}) copy-start(bf16[192,896]{1,0:T(8,128)(2,1)S(1)} %collective-permute-done.6) | copy-start | bytes 1032196
  74.7 30.9 %collective-permute-start.10 = (bf16[256,896]{1,0:T(8,128)(2,1)}, bf16[256,896]{1,0:T(8,128)(2,1)}, u32[]{:S(2)}, u32[]{:S(2)}) collective-permute-start(bf16[256,896]{1,0:T(8,128)(2,1)} %convolution_convert_fusion), channel_id=1, source_target_pairs={{0,4},{4,0},{8,12},{12,8},{16,20},{20,16},{24,28},{28,24},{1,5},{5... | collective-permute-start | bytes 1376264 | tf_op jit(solution)/shard_map/ppermute | solution.py:72
  103.3 2.3 %copy-start.5 = (bf16[192,896]{1,0:T(8,128)(2,1)S(1)}, bf16[192,896]{1,0:T(8,128)(2,1)}, u32[]{:S(2)}) copy-start(bf16[192,896]{1,0:T(8,128)(2,1)} %copy-done.4) | copy-start | bytes 1032196
where the time goes:
time: 110 us; the launch traced here: 109 us
  waiting for transfers between devices  35.7 us (32%)
  blocking collectives  34.6 us (31%)
  starting transfers between devices  24 us (22%)
  matrix products  8.79 us (8%)
  other arithmetic  3.76 us (3%)
  local copies, waits for them, and re-layouts  1.72 us (2%)
    psum x1, blocking collectives, on_device(): total = lax.psum(tokens, 'dp')  27.1 us
    ppermute x2, waiting for transfers between devices, on_device(): hq = lax.ppermute(h, 'dp', perm_z([(0, 2), (2, 0), (1, 3), (3, 1)]))  15.4 us
    ppermute x2, waiting for transfers between devices, on_device(): hf2 = lax.ppermute(hq, 'dp', perm_z([(1, 0), (2, 3)]))  11.1 us
    dot_general x4, matrix products, project(): lax.dot_general(cots, hs, (((0,), (0,)), ((), ())), preferred_element_typ...  8.79 us
    ppermute x2, starting transfers between devices, on_device(): ha = lax.ppermute(h, 'dp', perm_z([(0, 1), (1, 0), (2, 3), (3, 2)]))  8.11 us
    all_gather x1, blocking collectives, on_device(): cots = lax.all_gather(moved, 'mp', axis=0, tiled=True)  7.47 us
    ppermute x2, starting transfers between devices, on_device(): hq = lax.ppermute(h, 'dp', perm_z([(0, 2), (2, 0), (1, 3), (3, 1)]))  6.66 us
    ppermute x2, waiting for transfers between devices, on_device(): ha = lax.ppermute(h, 'dp', perm_z([(0, 1), (1, 0), (2, 3), (3, 2)]))  6.41 us
  transfers between devices with their start and end apart: 11, of which 4 were waited for; matrix products, arithmetic and copies ran while one was open for 7% of the time, Pallas kernels for 0%

commit v1 on v0

--- a/solution.py
+++ b/solution.py
@@ -42,7 +42,9 @@
             for m in range(mp):
                 perm.append(((a * inner + b) * mp + m, (m * inner + b) * mp + (a ^ m)))
     moved = lax.ppermute(scaled, both, perm)
-    cots = lax.all_gather(moved, "mp", axis=0, tiled=True)
+    cots = jnp.concatenate(
+        lax.all_to_all(jnp.stack([moved] * lax.axis_size("mp")), "mp", 0, 0), axis=0
+    )
     total = lax.psum(tokens, "dp")
 
     def perm_z(pairs):

time: 110 us -> 109 us (level)
  blocking collectives: 34.6 us -> 27.1 us
  waiting for transfers between devices: 35.7 us -> 40.9 us
    all_gather x1 -> x0, blocking collectives: 7.47 us -> none  [on_device(): cots = lax.all_gather(moved, 'mp', axis=0, tiled=True)]
    ppermute x1, waiting for transfers between devices: 2.82 us -> 6.77 us  [on_device(): moved = lax.ppermute(scaled, both, perm)]
    all_to_all x0 -> x1, starting transfers between devices: none -> 3.48 us  [on_device(): lax.all_to_all(jnp.stack([moved] * lax.axis_size('mp')), 'mp', 0, 0)]
    ppermute x2, starting transfers between devices: 8.11 us -> 5.13 us  [on_device(): ha = lax.ppermute(h, 'dp', perm_z([(0, 1), (1, 0), (2, 3), (3, 2)]))]
  transfers between devices with their start and end apart: 11 -> 12, of which waited for: 4 -> 5; matrix products, arithmetic and copies ran while one was open for 7% -> 8% of each run, Pallas kernels for 0% -> 0%
where the time goes in v1:
time: 109 us; the launch traced here: 108 us
  waiting for transfers between devices  40.9 us (38%)
  blocking collectives  27.1 us (25%)
  starting transfers between devices  24.5 us (22%)
  matrix products  8.62 us (8%)
  other arithmetic  3.84 us (4%)
  local copies, waits for them, and re-layouts  2.65 us (2%)
    psum x1, blocking collectives, on_device(): total = lax.psum(tokens, 'dp')  27.1 us
    ppermute x2, waiting for transfers between devices, on_device(): hq = lax.ppermute(h, 'dp', perm_z([(0, 2), (2, 0), (1, 3), (3, 1)]))  15.3 us
    ppermute x2, waiting for transfers between devices, on_device(): hf2 = lax.ppermute(hq, 'dp', perm_z([(1, 0), (2, 3)]))  11.4 us
    dot_general x4, matrix products, project(): lax.dot_general(cots, hs, (((0,), (0,)), ((), ())), preferred_element_typ...  8.62 us
    ppermute x2, waiting for transfers between devices, on_device(): ha = lax.ppermute(h, 'dp', perm_z([(0, 1), (1, 0), (2, 3), (3, 2)]))  7.44 us
    ppermute x1, waiting for transfers between devices, on_device(): moved = lax.ppermute(scaled, both, perm)  6.77 us
    ppermute x2, starting transfers between devices, on_device(): hq = lax.ppermute(h, 'dp', perm_z([(0, 2), (2, 0), (1, 3), (3, 1)]))  6.66 us
    ppermute x2, starting transfers between devices, on_device(): ha = lax.ppermute(h, 'dp', perm_z([(0, 1), (1, 0), (2, 3), (3, 2)]))  5.13 us
  transfers between devices with their start and end apart: 12, of which 5 were waited for; matrix products, arithmetic and copies ran while one was open for 8% of the time, Pallas kernels for 0%

profile of v1, /device:TPU:4, one launch (start us, length us, event | category | flops | bytes accessed | tf_op | source)
XLA Modules:
  0.0 108.4 jit_solution(750028796801393868)
XLA Ops:
  0.0 0.9 select_reduce_fusion
  0.9 0.1 reshape.69
  1.0 1.4 %fusion.24 = (bf16[1,3,64,896]{3,2,1,0:T(8,128)(2,1)S(1)}, bf16[1,3,64,896]{3,2,1,0:T(8,128)(2,1)S(1)}, bf16[1,3,64,896]{3,2,1,0:T(8,128)(2,1)S(1)}, bf16[1,3,64,896]{3,2,1,0:T(8,128)(2,1)S(1)}) fusion(bf16[1,3,64,1792]{3,2,1,0:T(8,128)(2,1)} %param.7, bf16[1,3,64,1792]{3,2,1,0:T(8,128)(2,1)} %param.8), kind=kLoop, calls=%fused_computation.45 | loop fusion | bytes 2752512 | tf_op jit(solution)/shard_map/slice | solution.py:58
  2.5 0.6 fusion.13
  3.1 2.7 %collective-permute-start.2 = (bf16[192,896]{1,0:T(8,128)(2,1)S(1)}, bf16[192,896]{1,0:T(8,128)(2,1)S(1)}, u32[]{:S(2)}, u32[]{:S(2)}) collective-permute-start(bf16[192,896]{1,0:T(8,128)(2,1)S(1)} %get-tuple-element.13), channel_id=1, source_target_pairs={{0,16},{4,20},{16,0},{20,4},{8,24},{12,28},{24,8},{28,12},{1,17},{... | collective-permute-start | bytes 1032200 | tf_op jit(solution)/shard_map/ppermute | solution.py:67
  6.4 0.7 multiply_reduce_fusion
  7.1 0.1 mul.73
  7.2 0.1 fusion.14
  7.3 0.1 maximum_select_fusion
  7.5 2.2 %collective-permute-start = (bf16[192,512]{1,0:T(8,128)(2,1)S(1)}, bf16[192,512]{1,0:T(8,128)(2,1)S(1)}, u32[]{:S(2)}, u32[]{:S(2)}) collective-permute-start(bf16[192,512]{1,0:T(8,128)(2,1)S(1)} %maximum_select_fusion), channel_id=1, source_target_pairs={{0,0},{1,9},{2,18},{3,27},{4,4},{5,13},{6,22},{7,31},{8,1},{9,8},{... | collective-permute-start | bytes 589832 | tf_op jit(solution)/shard_map/ppermute | solution.py:44
  9.7 0.7 collective-permute-start.3
  10.4 4.0 %collective-permute-start.7 = (bf16[192,896]{1,0:T(8,128)(2,1)S(1)}, bf16[192,896]{1,0:T(8,128)(2,1)}, u32[]{:S(2)}, u32[]{:S(2)}) collective-permute-start(bf16[192,896]{1,0:T(8,128)(2,1)S(1)} %get-tuple-element.14), channel_id=1, source_target_pairs={{0,16},{4,20},{16,0},{20,4},{8,24},{12,28},{24,8},{28,12},{1,17},{... | collective-permute-start | bytes 1032200 | tf_op jit(solution)/shard_map/ppermute | solution.py:67
  14.4 15.3 %collective-permute-done.2 = bf16[192,896]{1,0:T(8,128)(2,1)S(1)} collective-permute-done((bf16[192,896]{1,0:T(8,128)(2,1)S(1)}, bf16[192,896]{1,0:T(8,128)(2,1)S(1)}, u32[]{:S(2)}, u32[]{:S(2)}) %collective-permute-start.2) | collective-permute-done | bytes 344096 | tf_op jit(solution)/shard_map/ppermute | solution.py:67
  29.7 1.3 %collective-permute-start.4 = (bf16[192,896]{1,0:T(8,128)(2,1)S(1)}, bf16[192,896]{1,0:T(8,128)(2,1)S(1)}, u32[]{:S(2)}, u32[]{:S(2)}) collective-permute-start(bf16[192,896]{1,0:T(8,128)(2,1)S(1)} %collective-permute-done.2), channel_id=1, source_target_pairs={{8,0},{12,4},{16,24},{20,28},{9,1},{13,5},{17,25},{21,29},{10,2},{... | collective-permute-start | bytes 1032200 | tf_op jit(solution)/shard_map/ppermute | solution.py:69
  31.0 6.8 %collective-permute-done = bf16[192,512]{1,0:T(8,128)(2,1)S(1)} collective-permute-done((bf16[192,512]{1,0:T(8,128)(2,1)S(1)}, bf16[192,512]{1,0:T(8,128)(2,1)S(1)}, u32[]{:S(2)}, u32[]{:S(2)}) %collective-permute-start) | collective-permute-done | bytes 196640 | tf_op jit(solution)/shard_map/ppermute | solution.py:44
  37.8 0.9 stack.2
  38.7 3.5 %all-to-all-start = ((bf16[4,192,512]{2,1,0:T(8,128)(2,1)}), bf16[4,192,512]{2,1,0:T(8,128)(2,1)S(1)}, u32[]{:S(2)}, u32[]{:S(2)}) async-start(bf16[4,192,512]{2,1,0:T(8,128)(2,1)} %stack.2), calls=%async_computation | async-start | bytes 1572864 | tf_op jit(solution)/shard_map/all_to_all | solution.py:46
  42.2 0.3 collective-permute-start.1
  42.5 0.7 collective-permute-start.8
  43.2 4.8 %collective-permute-start.6 = (bf16[192,896]{1,0:T(8,128)(2,1)S(1)}, bf16[192,896]{1,0:T(8,128)(2,1)}, u32[]{:S(2)}, u32[]{:S(2)}) collective-permute-start(bf16[192,896]{1,0:T(8,128)(2,1)S(1)} %get-tuple-element.14), channel_id=1, source_target_pairs={{0,8},{4,12},{8,0},{12,4},{16,24},{20,28},{24,16},{28,20},{1,9},{5... | collective-permute-start | bytes 1032200 | tf_op jit(solution)/shard_map/ppermute | solution.py:66
  48.0 1.3 %collective-permute-start.9 = (bf16[192,896]{1,0:T(8,128)(2,1)}, bf16[192,896]{1,0:T(8,128)(2,1)S(1)}, u32[]{:S(2)}, u32[]{:S(2)}) collective-permute-start(bf16[192,896]{1,0:T(8,128)(2,1)} %collective-permute-done.7), channel_id=1, source_target_pairs={{8,0},{12,4},{16,24},{20,28},{9,1},{13,5},{17,25},{21,29},{10,2},{... | collective-permute-start | bytes 1032200 | tf_op jit(solution)/shard_map/ppermute | solution.py:69
  49.3 1.0 collective-permute-done.4
  50.4 7.4 %collective-permute-done.1 = bf16[192,896]{1,0:T(8,128)(2,1)} collective-permute-done((bf16[192,896]{1,0:T(8,128)(2,1)S(1)}, bf16[192,896]{1,0:T(8,128)(2,1)}, u32[]{:S(2)}, u32[]{:S(2)}) %collective-permute-start.1) | collective-permute-done | bytes 344096 | tf_op jit(solution)/shard_map/ppermute | solution.py:66
  57.8 2.3 %convolution_convert_fusion.1 = bf16[256,896]{1,0:T(8,128)(2,1)} fusion(bf16[768,512]{1,0:T(8,128)(2,1)S(1)} %bitcast.23, bf16[192,896]{1,0:T(8,128)(2,1)S(1)} %broadcast_select_fusion.1, bf16[192,896]{1,0:T(8,128)(2,1)S(1)} %collective-permute-done.2, bf16[192,896]{1,0:T(8,128)(2,1)} %collective-permute-done.1, bf16[192,896]{1,0:T(8,128)(2,1)S(1)} %get-tuple-element.13), kind=kOutput, calls=%fused_computation.8 | convolution fusion | flops 358055936 | bytes 2228224 | tf_op jit(solution)/shard_map/dot_general | solution.py:11
  60.2 1.5 %collective-permute-start.5 = (bf16[256,896]{1,0:T(8,128)(2,1)}, bf16[256,896]{1,0:T(8,128)(2,1)}, u32[]{:S(2)}, u32[]{:S(2)}) collective-permute-start(bf16[256,896]{1,0:T(8,128)(2,1)} %convolution_convert_fusion.1), channel_id=1, source_target_pairs={{0,4},{4,0},{8,12},{12,8},{16,20},{20,16},{24,28},{28,24},{1,5},{5... | collective-permute-start | bytes 1376264 | tf_op jit(solution)/shard_map/ppermute | solution.py:74
  61.7 10.4 %collective-permute-done.9 = bf16[192,896]{1,0:T(8,128)(2,1)S(1)} collective-permute-done((bf16[192,896]{1,0:T(8,128)(2,1)}, bf16[192,896]{1,0:T(8,128)(2,1)S(1)}, u32[]{:S(2)}, u32[]{:S(2)}) %collective-permute-start.9) | collective-permute-done | bytes 344096 | tf_op jit(solution)/shard_map/ppermute | solution.py:69
  72.1 1.7 %convolution_convert_fusion = bf16[256,896]{1,0:T(8,128)(2,1)S(1)} fusion(bf16[768,512]{1,0:T(8,128)(2,1)S(1)} %bitcast.24, bf16[192,896]{1,0:T(8,128)(2,1)S(1)} %broadcast_select_fusion, bf16[192,896]{1,0:T(8,128)(2,1)} %collective-permute-done.7, bf16[192,896]{1,0:T(8,128)(2,1)} %collective-permute-done.6, bf16[192,896]{1,0:T(8,128)(2,1)S(1)} %get-tuple-element.14), kind=kOutput, calls=%fused_computation.7 | convolution fusion | flops 358055936 | bytes 2228224 | tf_op jit(solution)/shard_map/dot_general | solution.py:11
  73.8 1.6 %collective-permute-start.10 = (bf16[256,896]{1,0:T(8,128)(2,1)S(1)}, bf16[256,896]{1,0:T(8,128)(2,1)S(1)}, u32[]{:S(2)}, u32[]{:S(2)}) collective-permute-start(bf16[256,896]{1,0:T(8,128)(2,1)S(1)} %convolution_convert_fusion), channel_id=1, source_target_pairs={{0,4},{4,0},{8,12},{12,8},{16,20},{20,16},{24,28},{28,24},{1,5},{5... | collective-permute-start | bytes 1376264 | tf_op jit(solution)/shard_map/ppermute | solution.py:74
  75.4 27.1 %psum.7 = f32[]{:T(128)} all-reduce(f32[]{:T(128)} %get-tuple-element.5), channel_id=1, replica_groups=mesh['dp'=8,'mp'=4] {'dp'}, use_global_device_ids=true, to_apply=%region_2.3 | all-reduce | flops 1 | bytes 8 | tf_op jit(solution)/shard_map/psum | solution.py:48
  102.5 2.4 %fusion.1 = f32[256,896]{1,0:T(8,128)S(1)} fusion(bf16[256,896]{1,0:T(8,128)(2,1)} %collective-permute-done.5, f32[]{:T(128)} %psum.7, bf16[768,512]{1,0:T(8,128)(2,1)S(1)} %bitcast.25, bf16[192,896]{1,0:T(8,128)(2,1)S(1)} %broadcast_select_fusion.1, bf16[192,896]{1,0:T(8,128)(2,1)} %copy-done.2, bf16[192,896]{1,0:T(8,128)(2,1)} %collective-permute-done.1, ...), kind=kOutput, calls=%fused_computation.6 | convolution fusion | flops 358514688 | bytes 3145732 | tf_op jit(solution)/shard_map/dot_general | solution.py:11
  104.9 2.2 %fusion = f32[256,896]{1,0:T(8,128)S(1)} fusion(bf16[256,896]{1,0:T(8,128)(2,1)S(1)} %collective-permute-done.10, f32[]{:T(128)} %psum.7, bf16[768,512]{1,0:T(8,128)(2,1)S(1)} %bitcast.26, bf16[192,896]{1,0:T(8,128)(2,1)S(1)} %broadcast_select_fusion, bf16[192,896]{1,0:T(8,128)(2,1)} %collective-permute-done.7, bf16[192,896]{1,0:T(8,128)(2,1)} %collective-permute-done.6, ...), kind=kOutput, calls=%fused_computation.4 | convolution fusion | flops 358514688 | bytes 3145732 | tf_op jit(solution)/shard_map/dot_general | solution.py:11
  107.1 1.4 %pad_maximum_fusion = f32[256,1792]{1,0:T(8,128)} fusion(f32[256,896]{1,0:T(8,128)S(1)} %fusion, f32[256,896]{1,0:T(8,128)S(1)} %fusion.1), kind=kLoop, calls=%fused_computation | loop fusion | flops 458752 | bytes 3670016 | tf_op jit(solution)/shard_map/concatenate | solution.py:81
  (19 shorter events, 0.3 us)
Async XLA Ops:
  1.0 5.4 %copy-start.1 = (s32[1,3]{1,0:T(1,128)S(1)}, s32[1,3]{1,0:T(1,128)}, u32[]{:S(2)}) copy-start(s32[1,3]{1,0:T(1,128)} %param.12) | copy-start | bytes 40
  1.0 6.2 %copy-start = (bf16[1,3,64,512]{3,2,1,0:T(8,128)(2,1)S(1)}, bf16[1,3,64,512]{3,2,1,0:T(8,128)(2,1)}, u32[]{:S(2)}) copy-start(bf16[1,3,64,512]{3,2,1,0:T(8,128)(2,1)} %param.9) | copy-start | bytes 589828
  3.1 26.6 %collective-permute-start.2 = (bf16[192,896]{1,0:T(8,128)(2,1)S(1)}, bf16[192,896]{1,0:T(8,128)(2,1)S(1)}, u32[]{:S(2)}, u32[]{:S(2)}) collective-permute-start(bf16[192,896]{1,0:T(8,128)(2,1)S(1)} %get-tuple-element.13), channel_id=1, source_target_pairs={{0,16},{4,20},{16,0},{20,4},{8,24},{12,28},{24,8},{28,12},{1,17},{... | collective-permute-start | bytes 1032200 | tf_op jit(solution)/shard_map/ppermute | solution.py:67
  7.5 30.3 %collective-permute-start = (bf16[192,512]{1,0:T(8,128)(2,1)S(1)}, bf16[192,512]{1,0:T(8,128)(2,1)S(1)}, u32[]{:S(2)}, u32[]{:S(2)}) collective-permute-start(bf16[192,512]{1,0:T(8,128)(2,1)S(1)} %maximum_select_fusion), channel_id=1, source_target_pairs={{0,0},{1,9},{2,18},{3,27},{4,4},{5,13},{6,22},{7,31},{8,1},{9,8},{... | collective-permute-start | bytes 589832 | tf_op jit(solution)/shard_map/ppermute | solution.py:44
  9.7 33.4 %collective-permute-start.3 = (bf16[192,896]{1,0:T(8,128)(2,1)S(1)}, bf16[192,896]{1,0:T(8,128)(2,1)S(1)}, u32[]{:S(2)}, u32[]{:S(2)}) collective-permute-start(bf16[192,896]{1,0:T(8,128)(2,1)S(1)} %get-tuple-element.13), channel_id=1, source_target_pairs={{8,16},{12,20},{16,8},{20,12},{9,17},{13,21},{17,9},{21,13},{10,18... | collective-permute-start | bytes 1032200 | tf_op jit(solution)/shard_map/ppermute | solution.py:68
  10.4 37.6 %collective-permute-start.7 = (bf16[192,896]{1,0:T(8,128)(2,1)S(1)}, bf16[192,896]{1,0:T(8,128)(2,1)}, u32[]{:S(2)}, u32[]{:S(2)}) collective-permute-start(bf16[192,896]{1,0:T(8,128)(2,1)S(1)} %get-tuple-element.14), channel_id=1, source_target_pairs={{0,16},{4,20},{16,0},{20,4},{8,24},{12,28},{24,8},{28,12},{1,17},{... | collective-permute-start | bytes 1032200 | tf_op jit(solution)/shard_map/ppermute | solution.py:67
  29.7 30.5 %copy-start.2 = (bf16[192,896]{1,0:T(8,128)(2,1)}, bf16[192,896]{1,0:T(8,128)(2,1)S(1)}, u32[]{:S(2)}) copy-start(bf16[192,896]{1,0:T(8,128)(2,1)S(1)} %collective-permute-done.2) | copy-start | bytes 1032196
  29.7 20.7 %collective-permute-start.4 = (bf16[192,896]{1,0:T(8,128)(2,1)S(1)}, bf16[192,896]{1,0:T(8,128)(2,1)S(1)}, u32[]{:S(2)}, u32[]{:S(2)}) collective-permute-start(bf16[192,896]{1,0:T(8,128)(2,1)S(1)} %collective-permute-done.2), channel_id=1, source_target_pairs={{8,0},{12,4},{16,24},{20,28},{9,1},{13,5},{17,25},{21,29},{10,2},{... | collective-permute-start | bytes 1032200 | tf_op jit(solution)/shard_map/ppermute | solution.py:69
  38.7 19.1 %all-to-all-start = ((bf16[4,192,512]{2,1,0:T(8,128)(2,1)}), bf16[4,192,512]{2,1,0:T(8,128)(2,1)S(1)}, u32[]{:S(2)}, u32[]{:S(2)}) async-start(bf16[4,192,512]{2,1,0:T(8,128)(2,1)} %stack.2), calls=%async_computation | async-start | bytes 1572864 | tf_op jit(solution)/shard_map/all_to_all | solution.py:46
  42.2 15.6 %collective-permute-start.1 = (bf16[192,896]{1,0:T(8,128)(2,1)S(1)}, bf16[192,896]{1,0:T(8,128)(2,1)}, u32[]{:S(2)}, u32[]{:S(2)}) collective-permute-start(bf16[192,896]{1,0:T(8,128)(2,1)S(1)} %get-tuple-element.13), channel_id=1, source_target_pairs={{0,8},{4,12},{8,0},{12,4},{16,24},{20,28},{24,16},{28,20},{1,9},{5... | collective-permute-start | bytes 1032200 | tf_op jit(solution)/shard_map/ppermute | solution.py:66
  42.5 19.2 %collective-permute-start.8 = (bf16[192,896]{1,0:T(8,128)(2,1)S(1)}, bf16[192,896]{1,0:T(8,128)(2,1)S(1)}, u32[]{:S(2)}, u32[]{:S(2)}) collective-permute-start(bf16[192,896]{1,0:T(8,128)(2,1)S(1)} %get-tuple-element.14), channel_id=1, source_target_pairs={{8,16},{12,20},{16,8},{20,12},{9,17},{13,21},{17,9},{21,13},{10,18... | collective-permute-start | bytes 1032200 | tf_op jit(solution)/shard_map/ppermute | solution.py:68
  43.2 29.0 %collective-permute-start.6 = (bf16[192,896]{1,0:T(8,128)(2,1)S(1)}, bf16[192,896]{1,0:T(8,128)(2,1)}, u32[]{:S(2)}, u32[]{:S(2)}) collective-permute-start(bf16[192,896]{1,0:T(8,128)(2,1)S(1)} %get-tuple-element.14), channel_id=1, source_target_pairs={{0,8},{4,12},{8,0},{12,4},{16,24},{20,28},{24,16},{28,20},{1,9},{5... | collective-permute-start | bytes 1032200 | tf_op jit(solution)/shard_map/ppermute | solution.py:66
  48.0 24.1 %collective-permute-start.9 = (bf16[192,896]{1,0:T(8,128)(2,1)}, bf16[192,896]{1,0:T(8,128)(2,1)S(1)}, u32[]{:S(2)}, u32[]{:S(2)}) collective-permute-start(bf16[192,896]{1,0:T(8,128)(2,1)} %collective-permute-done.7), channel_id=1, source_target_pairs={{8,0},{12,4},{16,24},{20,28},{9,1},{13,5},{17,25},{21,29},{10,2},{... | collective-permute-start | bytes 1032200 | tf_op jit(solution)/shard_map/ppermute | solution.py:69
  60.2 42.3 %collective-permute-start.5 = (bf16[256,896]{1,0:T(8,128)(2,1)}, bf16[256,896]{1,0:T(8,128)(2,1)}, u32[]{:S(2)}, u32[]{:S(2)}) collective-permute-start(bf16[256,896]{1,0:T(8,128)(2,1)} %convolution_convert_fusion.1), channel_id=1, source_target_pairs={{0,4},{4,0},{8,12},{12,8},{16,20},{20,16},{24,28},{28,24},{1,5},{5... | collective-permute-start | bytes 1376264 | tf_op jit(solution)/shard_map/ppermute | solution.py:74
  73.8 31.0 %collective-permute-start.10 = (bf16[256,896]{1,0:T(8,128)(2,1)S(1)}, bf16[256,896]{1,0:T(8,128)(2,1)S(1)}, u32[]{:S(2)}, u32[]{:S(2)}) collective-permute-start(bf16[256,896]{1,0:T(8,128)(2,1)S(1)} %convolution_convert_fusion), channel_id=1, source_target_pairs={{0,4},{4,0},{8,12},{12,8},{16,20},{20,16},{24,28},{28,24},{1,5},{5... | collective-permute-start | bytes 1376264 | tf_op jit(solution)/shard_map/ppermute | solution.py:74
